TPU v7x, 128 devices: a whole 4x4x4 slice. The times are simulated.
128 devices in a mesh: row: 64 (over z, y, x), col: 2 (over core).
Axes of the slice: x: 4, y: 4, z: 4, core: 2. Of those that a mesh axis runs over, the one named last changes fastest.
Arguments:
- matrix: float32 [12288, 12288], P('row', 'col'), may hold values from -2 to 2, as said below
- diagonal: float32 [12288], P(('row', 'col')), may hold values from 1 to 6
- start: float32 [12288], P(('row', 'col')), may hold values from -6 to 6
Outputs:
- basis: float32 [4, 12288], P(None, ('row', 'col'))
- coefficients: float32 [2, 3], replicated
Inputs may be any that keep to these rules, and one draw needn't show every extreme that they name: matrix is exactly symmetric, its entries of order one over the square root of 12288.
All inputs are finite; a program needn't handle non-finite values.
Results may differ from a plain program's by a relative error of at most 0.0003.
Values sent between devices are 32-bit elements.
No kernel may reach another device: no remote copies, remote signals or barrier semaphores. Data moves between devices by JAX's collectives and lax.ppermute only.
A program may use at most 64 MiB of HBM per device.

v0:
```python
import functools
import math

import jax
import jax.numpy as jnp
from jax import lax
from jax.sharding import Mesh
from jax.sharding import PartitionSpec as P

ITERS = 3
ROW = ("row_0", "row_1", "row_2")
ROW_COL = ("row_0", "row_1", "row_2", "col")


def over_axes(value, axes):
    return functools.reduce(lax.psum, axes, value)


def local(matrix, diagonal, start):
    rows_total = lax.axis_size(ROW)
    cols_total = lax.axis_size("col")
    tile_len = start.shape[0]
    full_dim = tile_len * rows_total * cols_total
    col_len = matrix.shape[1]
    col_idx = lax.axis_index("col")

    def apply_matrix(vector):
        gathered = lax.all_gather(vector, ROW_COL, axis=0, tiled=True)
        column = lax.dynamic_slice_in_dim(gathered, col_idx * col_len, col_len, 0)
        partial_value = jnp.dot(
            matrix, column, precision=lax.Precision.HIGHEST, preferred_element_type=jnp.float32
        )
        return (
            lax.psum_scatter(partial_value, "col", scatter_dimension=0, tiled=True)
            + diagonal * vector
        )

    start_sq = over_axes(jnp.sum(start * start), ROW_COL)
    current = start / jnp.sqrt(start_sq)
    basis_rows = jnp.zeros((ITERS + 1, tile_len), jnp.float32).at[0].set(current)
    alpha_list = []
    beta_list = []
    for iteration in range(ITERS):
        image = apply_matrix(current)
        local_intersect = jnp.dot(
            basis_rows, image, precision=lax.Precision.HIGHEST, preferred_element_type=jnp.float32
        )
        intersect, total_sq = (
            over_axes(local_intersect, ROW_COL),
            over_axes(jnp.sum(image * image), ROW_COL),
        )
        image = image - jnp.dot(
            intersect,
            basis_rows,
            precision=lax.Precision.HIGHEST,
            preferred_element_type=jnp.float32,
        )
        squared = total_sq - jnp.sum(intersect * intersect)
        beta_value = jnp.sqrt(squared)
        current = image / beta_value
        basis_rows = basis_rows.at[iteration + 1].set(current)
        alpha_list.append(intersect[iteration])
        beta_list.append(beta_value)
    coefficients = jnp.stack([jnp.stack(alpha_list), jnp.stack(beta_list)])
    return (basis_rows * jnp.float32(math.sqrt(full_dim)), coefficients)


def solution(mesh):
    split = Mesh(
        mesh.devices.reshape(4, 4, 4, mesh.shape["col"]), ("row_0", "row_1", "row_2", "col")
    )
    return jax.shard_map(
        local,
        mesh=split,
        in_specs=(P(ROW, "col"), P(ROW_COL), P(ROW_COL)),
        out_specs=(P(None, ROW_COL), P()),
        check_vma=False,
    )
```

profile of v0, /device:TPU:1, one launch (start us, length us, event | category | flops | bytes accessed | tf_op | source)
XLA Modules:
  0.0 365.5 jit_solution(11045711491770731486)
XLA Ops:
  0.6 0.0 copy-start.1
  0.6 0.0 copy-start
  0.7 1.3 multiply_reduce_fusion.6
  1.9 11.2 %psum.196 = f32[]{:T(128)} all-reduce(f32[]{:T(128)} %multiply_reduce_fusion.6), channel_id=1, replica_groups=mesh['row_0'=4,'row_1'=4,'row_2'=4,'col'=2] {'row_0'}, use_global_device_ids=true, to_apply=%region_1.0 | all-reduce | flops 1 | bytes 8 | tf_op jit(solution)/shard_map/psum | solution.py:16
  13.1 9.6 %psum.197 = f32[]{:T(128)} all-reduce(f32[]{:T(128)} %psum.196), channel_id=1, replica_groups=mesh['row_0'=4,'row_1'=4,'row_2'=4,'col'=2] {'row_1'}, use_global_device_ids=true, to_apply=%region_2.0 | all-reduce | flops 1 | bytes 8 | tf_op jit(solution)/shard_map/psum | solution.py:16
  22.7 9.1 %psum.198 = f32[]{:T(128)} all-reduce(f32[]{:T(128)} %psum.197), channel_id=1, replica_groups=mesh['row_0'=4,'row_1'=4,'row_2'=4,'col'=2] {'row_2'}, use_global_device_ids=true, to_apply=%region_3.0 | all-reduce | flops 1 | bytes 8 | tf_op jit(solution)/shard_map/psum | solution.py:16
  31.8 9.2 %psum.199 = f32[]{:T(128)} all-reduce(f32[]{:T(128)} %psum.198), channel_id=1, replica_groups=mesh['row_0'=4,'row_1'=4,'row_2'=4,'col'=2] {'col'}, use_global_device_ids=true, to_apply=%region_4.0 | all-reduce | flops 1 | bytes 8 | tf_op jit(solution)/shard_map/psum | solution.py:16
  41.7 0.8 fusion.17
  42.5 62.1 %all-reduce.1 = f32[12288]{0:T(1024)S(1)} all-reduce(f32[12288]{0:T(1024)S(1)} %get-tuple-element.80), channel_id=1, replica_groups=mesh['row_0'=4,'row_1'=4,'row_2'=4,'col'=2] {'row_0','row_1','row_2','col'}, use_global_device_ids=true, to_apply=%add.1 | all-reduce | flops 12288 | bytes 98304
  104.5 5.5 %fusion.18 = f32[1,192]{1,0:T(1,128)S(1)} fusion(f32[6144,1]{0,1:T(1,128)S(1)} %bitcast.75, f32[192,6144]{1,0:T(8,128)} %param.11), kind=kOutput, calls=%fused_computation.39 | convolution fusion | flops 14155776 | bytes 4743936 | tf_op jit(solution)/shard_map/dot_general | solution.py:30
  110.1 2.8 all-reduce.4
  112.8 0.0 copy-done.1
  112.8 0.6 dynamic-slice.31
  114.1 0.0 copy-done
  114.1 0.7 multiply_reduce_fusion.5
  114.8 0.1 convolution_bitcast_fusion.5
  114.9 8.6 %all-reduce.15 = (f32[4]{0:T(128)S(1)}, f32[]{:T(128)}) all-reduce(f32[4]{0:T(128)S(1)} %convolution_bitcast_fusion.5, f32[]{:T(128)} %get-tuple-element.78), channel_id=1, replica_groups=mesh['row_0'=4,'row_1'=4,'row_2'=4,'col'=2] {'row_0'}, use_global_device_ids=true, to_apply=%region_6.0 | all-reduce | flops 5 | bytes 40 | tf_op jit(solution)/shard_map/psum | solution.py:16
  123.5 7.3 %all-reduce.12 = (f32[4]{0:T(128)S(1)}, f32[]{:T(128)}) all-reduce(f32[4]{0:T(128)S(1)} %get-tuple-element.66, f32[]{:T(128)} %get-tuple-element.67), channel_id=1, replica_groups=mesh['row_0'=4,'row_1'=4,'row_2'=4,'col'=2] {'row_1'}, use_global_device_ids=true, to_apply=%region_7.0 | all-reduce | flops 5 | bytes 40 | tf_op jit(solution)/shard_map/psum | solution.py:16
  130.8 7.5 %all-reduce.9 = (f32[4]{0:T(128)S(1)}, f32[]{:T(128)}) all-reduce(f32[4]{0:T(128)S(1)} %get-tuple-element.60, f32[]{:T(128)} %get-tuple-element.61), channel_id=1, replica_groups=mesh['row_0'=4,'row_1'=4,'row_2'=4,'col'=2] {'row_2'}, use_global_device_ids=true, to_apply=%region_8.0 | all-reduce | flops 5 | bytes 40 | tf_op jit(solution)/shard_map/psum | solution.py:16
  138.3 9.1 %all-reduce.18 = (f32[4]{0:T(128)S(1)}, f32[]{:T(128)}) all-reduce(f32[4]{0:T(128)S(1)} %get-tuple-element.54, f32[]{:T(128)} %get-tuple-element.55), channel_id=1, replica_groups=mesh['row_0'=4,'row_1'=4,'row_2'=4,'col'=2] {'col'}, use_global_device_ids=true, to_apply=%region_9.0 | all-reduce | flops 5 | bytes 40 | tf_op jit(solution)/shard_map/psum | solution.py:16
  147.3 0.6 multiply_reduce_fusion.4
  149.3 0.1 fusion.1
  149.4 0.3 dynamic-update-slice.13
  149.7 62.6 %all-reduce.2 = f32[12288]{0:T(1024)S(1)} all-reduce(f32[12288]{0:T(1024)S(1)} %dynamic-update-slice.13), channel_id=1, replica_groups=mesh['row_0'=4,'row_1'=4,'row_2'=4,'col'=2] {'row_0','row_1','row_2','col'}, use_global_device_ids=true, to_apply=%add.2 | all-reduce | flops 12288 | bytes 98304
  212.3 5.5 %fusion.19 = f32[1,192]{1,0:T(1,128)S(1)} fusion(f32[6144,1]{0,1:T(1,128)S(1)} %bitcast.76, f32[192,6144]{1,0:T(8,128)} %param.11), kind=kOutput, calls=%fused_computation.40 | convolution fusion | flops 14155776 | bytes 4743936 | tf_op jit(solution)/shard_map/dot_general | solution.py:30
  217.8 2.8 all-reduce.5
  220.6 0.7 multiply_reduce_fusion.3
  221.3 0.1 convolution_bitcast_fusion.3
  221.4 7.9 %all-reduce.14 = (f32[4]{0:T(128)S(1)}, f32[]{:T(128)}) all-reduce(f32[4]{0:T(128)S(1)} %convolution_bitcast_fusion.3, f32[]{:T(128)} %get-tuple-element.76), channel_id=1, replica_groups=mesh['row_0'=4,'row_1'=4,'row_2'=4,'col'=2] {'row_0'}, use_global_device_ids=true, to_apply=%region_17.0 | all-reduce | flops 5 | bytes 40 | tf_op jit(solution)/shard_map/psum | solution.py:16
  229.4 8.0 %all-reduce.11 = (f32[4]{0:T(128)S(1)}, f32[]{:T(128)}) all-reduce(f32[4]{0:T(128)S(1)} %get-tuple-element.64, f32[]{:T(128)} %get-tuple-element.65), channel_id=1, replica_groups=mesh['row_0'=4,'row_1'=4,'row_2'=4,'col'=2] {'row_1'}, use_global_device_ids=true, to_apply=%region_18.0 | all-reduce | flops 5 | bytes 40 | tf_op jit(solution)/shard_map/psum | solution.py:16
  237.3 6.8 %all-reduce.8 = (f32[4]{0:T(128)S(1)}, f32[]{:T(128)}) all-reduce(f32[4]{0:T(128)S(1)} %get-tuple-element.58, f32[]{:T(128)} %get-tuple-element.59), channel_id=1, replica_groups=mesh['row_0'=4,'row_1'=4,'row_2'=4,'col'=2] {'row_2'}, use_global_device_ids=true, to_apply=%region_19.0 | all-reduce | flops 5 | bytes 40 | tf_op jit(solution)/shard_map/psum | solution.py:16
  244.2 9.1 %all-reduce.17 = (f32[4]{0:T(128)S(1)}, f32[]{:T(128)}) all-reduce(f32[4]{0:T(128)S(1)} %get-tuple-element.52, f32[]{:T(128)} %get-tuple-element.53), channel_id=1, replica_groups=mesh['row_0'=4,'row_1'=4,'row_2'=4,'col'=2] {'col'}, use_global_device_ids=true, to_apply=%region_20.0 | all-reduce | flops 5 | bytes 40 | tf_op jit(solution)/shard_map/psum | solution.py:16
  253.3 0.7 multiply_reduce_fusion.2
  255.4 0.1 fusion.3
  255.5 0.3 dynamic-update-slice.14
  255.8 63.2 %all-reduce.3 = f32[12288]{0:T(1024)S(1)} all-reduce(f32[12288]{0:T(1024)S(1)} %dynamic-update-slice.14), channel_id=1, replica_groups=mesh['row_0'=4,'row_1'=4,'row_2'=4,'col'=2] {'row_0','row_1','row_2','col'}, use_global_device_ids=true, to_apply=%add.3 | all-reduce | flops 12288 | bytes 98304
  319.0 5.5 %fusion.20 = f32[1,192]{1,0:T(1,128)S(1)} fusion(f32[6144,1]{0,1:T(1,128)S(1)} %bitcast.74, f32[192,6144]{1,0:T(8,128)} %param.11), kind=kOutput, calls=%fused_computation.41 | convolution fusion | flops 14155776 | bytes 4743936 | tf_op jit(solution)/shard_map/dot_general | solution.py:30
  324.5 3.0 all-reduce.6
  327.6 0.7 multiply_reduce_fusion.1
  328.3 0.1 convolution_bitcast_fusion.1
  328.4 7.1 %all-reduce.13 = (f32[4]{0:T(128)S(1)}, f32[]{:T(128)}) all-reduce(f32[4]{0:T(128)S(1)} %convolution_bitcast_fusion.1, f32[]{:T(128)} %get-tuple-element.74), channel_id=1, replica_groups=mesh['row_0'=4,'row_1'=4,'row_2'=4,'col'=2] {'row_0'}, use_global_device_ids=true, to_apply=%region_28.0 | all-reduce | flops 5 | bytes 40 | tf_op jit(solution)/shard_map/psum | solution.py:16
  335.5 8.7 %all-reduce.10 = (f32[4]{0:T(128)S(1)}, f32[]{:T(128)}) all-reduce(f32[4]{0:T(128)S(1)} %get-tuple-element.62, f32[]{:T(128)} %get-tuple-element.63), channel_id=1, replica_groups=mesh['row_0'=4,'row_1'=4,'row_2'=4,'col'=2] {'row_1'}, use_global_device_ids=true, to_apply=%region_29.0 | all-reduce | flops 5 | bytes 40 | tf_op jit(solution)/shard_map/psum | solution.py:16
  344.2 6.7 %all-reduce.7 = (f32[4]{0:T(128)S(1)}, f32[]{:T(128)}) all-reduce(f32[4]{0:T(128)S(1)} %get-tuple-element.56, f32[]{:T(128)} %get-tuple-element.57), channel_id=1, replica_groups=mesh['row_0'=4,'row_1'=4,'row_2'=4,'col'=2] {'row_2'}, use_global_device_ids=true, to_apply=%region_30.0 | all-reduce | flops 5 | bytes 40 | tf_op jit(solution)/shard_map/psum | solution.py:16
  350.9 8.8 %all-reduce.16 = (f32[4]{0:T(128)S(1)}, f32[]{:T(128)}) all-reduce(f32[4]{0:T(128)S(1)} %get-tuple-element.50, f32[]{:T(128)} %get-tuple-element.51), channel_id=1, replica_groups=mesh['row_0'=4,'row_1'=4,'row_2'=4,'col'=2] {'col'}, use_global_device_ids=true, to_apply=%region_31.0 | all-reduce | flops 5 | bytes 40 | tf_op jit(solution)/shard_map/psum | solution.py:16
  359.7 0.7 multiply_reduce_fusion
  361.7 0.6 slice.70
  362.3 0.6 slice.69
  362.9 1.3 maximum_bitcast_fusion
  364.1 0.6 pad_maximum_fusion
  364.7 0.1 fusion.6
  364.9 0.6 broadcast_multiply_fusion
  (10 shorter events, 0.1 us)
Async XLA Ops:
  0.6 112.2 %copy-start.1 = (u32[128]{0:T(128)S(1)}, u32[128]{0:T(128)}, u32[]{:S(2)}) copy-start(u32[128]{0:T(128)} %constant.143) | copy-start | bytes 1540
  0.6 113.4 %copy-start = (f32[96]{0:T(128)S(1)}, f32[96]{0:T(128)}, u32[]{:S(2)}) copy-start(f32[96]{0:T(128)} %param.12) | copy-start | bytes 1156
where the time goes:
time: 366 us; the launch traced here: 365 us
  blocking collectives  331 us (90%)
  matrix products  17.4 us (5%)
  other arithmetic  8.45 us (2%)
  between operations  6.08 us (2%)
    unnamed x6, blocking collectives  196 us
    psum x16, blocking collectives, over_axes(): return functools.reduce(lax.psum, axes, value)  135 us
    dot_general x3, matrix products, apply_matrix(): jnp.dot(matrix, column, precision=lax.Precision.HIGHEST, preferred_elemen...  16.6 us

commit v1 on v0

v1 whole, which is shorter than its diff:
```python
import functools
import math

import jax
import jax.numpy as jnp
from jax import lax
from jax.experimental import pallas as pl
from jax.experimental.pallas import tpu as pltpu
from jax.sharding import Mesh
from jax.sharding import PartitionSpec as P

ITERS = 3
LANES = 128
ROW = ("row_0", "row_1", "row_2")
ROW_COL = ("row_0", "row_1", "row_2", "col")


def total(x):
    return jnp.sum(x, axis=(0, 1), keepdims=True)


def lane_of(shape):
    return lax.broadcasted_iota(jnp.int32, shape, 1)


def join_96(parts):
    s0, s1, s2, s3 = parts
    lane = lane_of(s0.shape)
    r1 = pltpu.roll(s1, 96, 1)
    r2 = pltpu.roll(s2, 64, 1)
    r3 = pltpu.roll(s3, 32, 1)
    return jnp.concatenate(
        [jnp.where(lane < 96, s0, r1), jnp.where(lane < 64, r1, r2), jnp.where(lane < 32, r2, r3)], axis=0
    )


def join_192(a0, a1, b0, b1):
    lane = lane_of(a0.shape)
    r0 = pltpu.roll(b0, 64, 1)
    r1 = pltpu.roll(b1, 64, 1)
    return jnp.concatenate([a0, jnp.where(lane < 64, a1, r0), jnp.where(lane < 64, r0, r1)], axis=0)


def gathered_image(g_ref, groups):
    def rows(first):
        return g_ref[pl.ds(first, groups, stride=8), :]

    return join_192(
        rows(0) + rows(2), rows(1) + rows(3), rows(4) + rows(6), rows(5) + rows(7)
    )


def product(vec, scale, m_ref, half_ref, pay_ref):
    groups = vec.shape[0] // 3
    half = groups // 2
    first = lax.axis_index("col") == 0
    for k in range(3):
        lo = vec[k * groups : k * groups + half]
        hi = vec[k * groups + half : (k + 1) * groups]
        half_ref[k * half : (k + 1) * half, :] = jnp.where(first, lo, hi)
    rows = m_ref.shape[0]
    acc = jnp.zeros((rows, LANES), jnp.float32)
    for t in range(m_ref.shape[1] // LANES):
        v = half_ref[pl.ds((t % 3) * half + t // 3, 1), :]
        acc = acc + m_ref[:, t * LANES : (t + 1) * LANES] * v
    top = jnp.sum(acc[:LANES].T, axis=0, keepdims=True)
    low = jnp.concatenate([acc[LANES:], jnp.zeros((2 * LANES - rows, LANES), jnp.float32)], axis=0)
    bottom = jnp.sum(low.T, axis=0, keepdims=True)
    even = lax.broadcasted_iota(jnp.int32, (8, LANES), 0) % 2 == 0
    tile = jnp.where(even, top, bottom) / scale
    for i in range(pay_ref.shape[0] // 8):
        pay_ref[8 * i : 8 * i + 8, :] = tile


def first_kernel(g_ref, m_ref, q_ref, d_ref, pay_ref, half_ref):
    groups = g_ref.shape[0] // 8
    start = join_96([g_ref[pl.ds(2 * j, groups, stride=8), :] for j in range(4)])
    d_ref[...] = join_96([g_ref[pl.ds(2 * j + 1, groups, stride=8), :] for j in range(4)])
    norm = jnp.sqrt(total(start * start))
    q_ref[...] = start / norm
    product(start, norm, m_ref, half_ref, pay_ref)


def orthogonal(g_ref, q_refs, d_ref):
    groups = g_ref.shape[0] // 8
    image = gathered_image(g_ref, groups) + d_ref[...] * q_refs[-1][...]
    dots = [total(q[...] * image) for q in q_refs]
    for h, q in zip(dots, q_refs):
        image = image - h * q[...]
    return image, dots[-1], jnp.sqrt(total(image * image))


def put(coef, row, col, value):
    shape = coef.shape
    at = (lax.broadcasted_iota(jnp.int32, shape, 0) == row) & (lane_of(shape) == col)
    return jnp.where(at, value, coef)


def middle_kernel(k, *refs):
    q_refs = refs[: k + 1]
    d_ref, g_ref, c_ref, m_ref, next_ref, c_out, pay_ref, half_ref = refs[k + 1 :]
    image, alpha, beta = orthogonal(g_ref, q_refs, d_ref)
    next_ref[...] = image / beta
    c_out[...] = put(put(c_ref[...], 0, k, alpha), 1, k, beta)
    product(image, beta, m_ref, half_ref, pay_ref)


def last_kernel(k, full_dim, *refs):
    q_refs = refs[: k + 1]
    d_ref, g_ref, c_ref, basis_ref, c_out, last_ref, piece_ref = refs[k + 1 :]
    image, alpha, beta = orthogonal(g_ref, q_refs, d_ref)
    last_ref[...] = image / beta
    coef = put(put(c_ref[...], 0, k, alpha), 1, k, beta)
    c_out[...] = coef[: c_out.shape[0], : c_out.shape[1]]
    groups = image.shape[0] // 3
    index = lax.axis_index(ROW_COL)
    group = index // 4
    place = index % 4
    for j in range(3):
        for v, q in enumerate((*q_refs, last_ref)):
            piece_ref[8 * j + v : 8 * j + v + 1, :] = q[pl.ds(j * groups + group, 1), :]
    a, b, c = piece_ref[0:8, :], piece_ref[8:16, :], piece_ref[16:24, :]
    lane = lane_of(a.shape)
    one = jnp.where(lane < 32, pltpu.roll(a, 32, 1), pltpu.roll(b, 32, 1))
    two = jnp.where(lane < 64, pltpu.roll(b, 64, 1), pltpu.roll(c, 64, 1))
    three = pltpu.roll(c, 96, 1)
    out = jnp.where(place == 0, a, jnp.where(place == 1, one, jnp.where(place == 2, two, three)))
    out = out * jnp.float32(math.sqrt(full_dim))
    basis_ref[...] = out[: basis_ref.shape[0], : basis_ref.shape[1]]


def call(body, outs, scratch, *args):
    vmem = pl.BlockSpec(memory_space=pltpu.VMEM)
    return pl.pallas_call(
        body,
        out_shape=[jax.ShapeDtypeStruct(s, jnp.float32) for s in outs],
        in_specs=[vmem] * len(args),
        out_specs=[vmem] * len(outs),
        scratch_shapes=[pltpu.VMEM(s, jnp.float32) for s in scratch],
        compiler_params=pltpu.CompilerParams(vmem_limit_bytes=16 << 20),
    )(*args)


def exchange(payload):
    return lax.all_to_all(payload, ROW_COL, 0, 0, tiled=True)


def local(matrix, diagonal, start):
    devices = lax.axis_size(ROW_COL)
    tile_len = start.shape[0]
    full_dim = tile_len * devices
    dense = (full_dim // LANES, LANES)
    half = (full_dim // LANES // 2, LANES)
    pay = (2 * devices, LANES)
    pair = jnp.pad(jnp.stack([start, diagonal]), ((0, 0), (0, LANES - tile_len)))
    gathered = exchange(jnp.broadcast_to(pair[None], (devices, 2, LANES)).reshape(pay))
    q, diag, payload = call(first_kernel, [dense, dense, pay], [half], gathered, matrix)
    basis = [q]
    coef = jnp.zeros((8, LANES), jnp.float32)
    for k in range(ITERS - 1):
        gathered = exchange(payload)
        q, coef, payload = call(
            functools.partial(middle_kernel, k),
            [dense, (8, LANES), pay],
            [half],
            *basis,
            diag,
            gathered,
            coef,
            matrix,
        )
        basis.append(q)
    gathered = exchange(payload)
    return tuple(
        call(
            functools.partial(last_kernel, ITERS - 1, full_dim),
            [(ITERS + 1, tile_len), (2, ITERS)],
            [dense, (24, LANES)],
            *basis,
            diag,
            gathered,
            coef,
        )
    )


def solution(mesh):
    split = Mesh(
        mesh.devices.reshape(4, 4, 4, mesh.shape["col"]), ("row_0", "row_1", "row_2", "col")
    )
    return jax.shard_map(
        local,
        mesh=split,
        in_specs=(P(ROW, "col"), P(ROW_COL), P(ROW_COL)),
        out_specs=(P(None, ROW_COL), P()),
        check_vma=False,
    )
```

time: 366 us -> 72.1 us (0.20)
  blocking collectives: 331 us -> 65 us
  matrix products: 17.4 us -> 0 us
  other arithmetic: 8.45 us -> 0.68 us
  between operations: 6.08 us -> 0.66 us
    unnamed x6 -> x0, blocking collectives: 196 us -> none
    psum x16 -> x0, blocking collectives: 135 us -> none  [over_axes(): return functools.reduce(lax.psum, axes, value)]
    all_to_all x0 -> x4, blocking collectives: none -> 65 us  [exchange(): return lax.all_to_all(payload, ROW_COL, 0, 0, tiled=True)]
    dot_general x9 -> x0, matrix products: 17.4 us -> none  [the longest x3 16.6 us: apply_matrix(): jnp.dot(matrix, column, precision=lax.Precision.HIGHEST, preferred_elemen...]
    reduce_sum x7 -> x0, other arithmetic: 5.24 us -> none  [the longest x3 2.02 us: local(): jnp.sum(image * image)]
where the time goes in v1:
time: 72.1 us; the launch traced here: 71.8 us
  blocking collectives  65 us (90%)
  Pallas kernels  3.16 us (4%)
  local copies, waits for them, and re-layouts  2.38 us (3%)
    all_to_all x4, blocking collectives, exchange(): return lax.all_to_all(payload, ROW_COL, 0, 0, tiled=True)  65 us
    pallas_call x4, Pallas kernels, call(): pl.pallas_call(body, out_shape=[jax.ShapeDtypeStruct(s, jnp.float32) for...  3.16 us
    unnamed x4, local copies, waits for them, and re-layouts  2.34 us

profile of v1, /device:TPU:1, one launch (start us, length us, event | category | flops | bytes accessed | tf_op | source)
XLA Modules:
  0.0 71.8 jit_solution(16800238698773662774)
XLA Ops:
  0.6 0.7 select_maximum_fusion
  1.4 21.7 %all_to_all.41 = f32[128,2,128]{2,1,0:T(2,128)S(1)} all-to-all(f32[128,2,128]{2,1,0:T(2,128)S(1)} %broadcast_in_dim.4), channel_id=1, replica_groups=mesh['row_0'=4,'row_1'=4,'row_2'=4,'col'=2] {'row_0','row_1','row_2','col'}, dimensions={0} | all-to-all | bytes 262144 | tf_op jit(solution)/shard_map/all_to_all | solution.py:145
  23.0 0.0 copy-start
  23.0 2.3 %copy-done = f32[192,6144]{1,0:T(8,128)S(1)} copy-done((f32[192,6144]{1,0:T(8,128)S(1)}, f32[192,6144]{1,0:T(8,128)}, u32[]{:S(2)}) %copy-start) | copy-done | bytes 4718616
  25.4 0.0 copy-start.1
  25.4 0.5 shard_map.50
  25.9 14.4 %all_to_all.42 = f32[128,2,128]{2,1,0:T(2,128)S(1)} all-to-all(f32[128,2,128]{2,1,0:T(2,128)S(1)} %bitcast.15), channel_id=1, replica_groups=mesh['row_0'=4,'row_1'=4,'row_2'=4,'col'=2] {'row_0','row_1','row_2','col'}, dimensions={0} | all-to-all | bytes 262144 | tf_op jit(solution)/shard_map/all_to_all | solution.py:145
  40.3 0.0 copy-done.1
  40.3 0.8 %shard_map.51 = (f32[96,128]{1,0:T(8,128)S(1)}, f32[8,128]{1,0:T(8,128)S(1)}, f32[256,128]{1,0:T(8,128)S(1)}) custom-call(f32[96,128]{1,0:T(8,128)S(1)} %get-tuple-element.11.refs_0_, f32[96,128]{1,0:T(8,128)S(1)} %get-tuple-element.12.refs_1_.refs_2_.refs_3_, f32[256,128]{1,0:T(8,128)S(1)} %bitcast.9, f32[8,128]{1,0:T(8,128)S(1)} %broadcast_in_dim.10.refs_3_, ...), custom_call_target="tpu_custom_call" | custom-call | tf_op jit(solution)/shard_map/pallas_call | solution.py:134
  41.1 14.4 %all_to_all.43 = f32[128,2,128]{2,1,0:T(2,128)S(1)} all-to-all(f32[128,2,128]{2,1,0:T(2,128)S(1)} %bitcast.13), channel_id=1, replica_groups=mesh['row_0'=4,'row_1'=4,'row_2'=4,'col'=2] {'row_0','row_1','row_2','col'}, dimensions={0} | all-to-all | bytes 262144 | tf_op jit(solution)/shard_map/all_to_all | solution.py:145
  55.6 0.8 %shard_map.52 = (f32[96,128]{1,0:T(8,128)S(1)}, f32[8,128]{1,0:T(8,128)S(1)}, f32[256,128]{1,0:T(8,128)S(1)}) custom-call(f32[96,128]{1,0:T(8,128)S(1)} %get-tuple-element.11.refs_0_, f32[96,128]{1,0:T(8,128)S(1)} %get-tuple-element.14.refs_1_, f32[96,128]{1,0:T(8,128)S(1)} %get-tuple-element.12.refs_1_.refs_2_.refs_3_, f32[256,128]{1,0:T(8,128)S(1)} %bitcast.10, ...), custom_call_target="tpu_custom_call" | custom-call | tf_op jit(solution)/shard_map/pallas_call | solution.py:134
  56.4 14.4 %all_to_all.44 = f32[128,2,128]{2,1,0:T(2,128)S(1)} all-to-all(f32[128,2,128]{2,1,0:T(2,128)S(1)} %bitcast.14), channel_id=1, replica_groups=mesh['row_0'=4,'row_1'=4,'row_2'=4,'col'=2] {'row_0','row_1','row_2','col'}, dimensions={0} | all-to-all | bytes 262144 | tf_op jit(solution)/shard_map/all_to_all | solution.py:145
  70.8 1.0 %shard_map.53 = (f32[4,96]{1,0:T(4,128)}, f32[2,3]{1,0:T(2,128)}) custom-call(f32[96,128]{1,0:T(8,128)S(1)} %get-tuple-element.11.refs_0_, f32[96,128]{1,0:T(8,128)S(1)} %get-tuple-element.14.refs_1_, f32[96,128]{1,0:T(8,128)S(1)} %get-tuple-element.17.refs_2_, f32[96,128]{1,0:T(8,128)S(1)} %get-tuple-element.12.refs_1_.refs_2_.refs_3_, ...), custom_call_target="tpu_custom_call" | custom-call | tf_op jit(solution)/shard_map/pallas_call | solution.py:134
  (2 shorter events, 0.0 us)
Async XLA Ops:
  23.0 2.3 %copy-start = (f32[192,6144]{1,0:T(8,128)S(1)}, f32[192,6144]{1,0:T(8,128)}, u32[]{:S(2)}) copy-start(f32[192,6144]{1,0:T(8,128)} %refs_5_.1) | copy-start | bytes 14155780
  25.4 15.0 %copy-start.1 = (f32[192,6144]{1,0:T(8,128)S(1)}, f32[192,6144]{1,0:T(8,128)}, u32[]{:S(2)}) copy-start(f32[192,6144]{1,0:T(8,128)} %refs_5_.1) | copy-start | bytes 14155780

commit v2 on v1

--- a/solution.py
+++ b/solution.py
@@ -68,6 +68,25 @@
     bottom = jnp.sum(low.T, axis=0, keepdims=True)
     even = lax.broadcasted_iota(jnp.int32, (8, LANES), 0) % 2 == 0
     tile = jnp.where(even, top, bottom) / scale
+    for i in range(pay_ref.shape[0] // 8):
+        pay_ref[8 * i : 8 * i + 8, :] = tile
+
+
+def pair_kernel(s_ref, d_ref, _, pay_ref, s_got, d_got, pair_ref, sems):
+    copies = [
+        pltpu.make_async_copy(s_ref, s_got, sems.at[0]),
+        pltpu.make_async_copy(d_ref, d_got, sems.at[1]),
+    ]
+    for copy in copies:
+        copy.start()
+    pair_ref[...] = jnp.zeros(pair_ref.shape, jnp.float32)
+    for copy in copies:
+        copy.wait()
+    width = s_got.shape[1]
+    pair_ref[0:1, 0:width] = s_got[...]
+    pair_ref[1:2, 0:width] = d_got[...]
+    even = lax.broadcasted_iota(jnp.int32, (8, LANES), 0) % 2 == 0
+    tile = jnp.where(even, pair_ref[0:1, :], pair_ref[1:2, :])
     for i in range(pay_ref.shape[0] // 8):
         pay_ref[8 * i : 8 * i + 8, :] = tile
 
@@ -141,6 +160,25 @@
     )(*args)
 
 
+def pair_call(pay, start, diagonal, matrix):
+    hbm = pl.BlockSpec(memory_space=pltpu.HBM)
+    cost = pl.CostEstimate(flops=0, transcendentals=0, bytes_accessed=4 * matrix.nbytes)
+    return pl.pallas_call(
+        pair_kernel,
+        out_shape=jax.ShapeDtypeStruct(pay, jnp.float32),
+        in_specs=[hbm] * 3,
+        out_specs=pl.BlockSpec(memory_space=pltpu.VMEM),
+        scratch_shapes=[
+            pltpu.VMEM(start.shape, jnp.float32),
+            pltpu.VMEM(diagonal.shape, jnp.float32),
+            pltpu.VMEM((8, LANES), jnp.float32),
+            pltpu.SemaphoreType.DMA((2,)),
+        ],
+        cost_estimate=cost,
+        compiler_params=pltpu.CompilerParams(vmem_limit_bytes=16 << 20),
+    )(*(pltpu.with_memory_space_constraint(x, pltpu.HBM) for x in (start, diagonal, matrix)))
+
+
 def exchange(payload):
     return lax.all_to_all(payload, ROW_COL, 0, 0, tiled=True)
 
@@ -152,8 +190,8 @@
     dense = (full_dim // LANES, LANES)
     half = (full_dim // LANES // 2, LANES)
     pay = (2 * devices, LANES)
-    pair = jnp.pad(jnp.stack([start, diagonal]), ((0, 0), (0, LANES - tile_len)))
-    gathered = exchange(jnp.broadcast_to(pair[None], (devices, 2, LANES)).reshape(pay))
+    payload = pair_call(pay, start.reshape(1, -1), diagonal.reshape(1, -1), matrix)
+    gathered = exchange(payload)
     q, diag, payload = call(first_kernel, [dense, dense, pay], [half], gathered, matrix)
     basis = [q]
     coef = jnp.zeros((8, LANES), jnp.float32)

time: 72.1 us -> 70 us (0.971)
  local copies, waits for them, and re-layouts: 2.38 us -> 0.01 us
  Pallas kernels: 3.16 us -> 4.14 us
    unnamed x4 -> x2, local copies, waits for them, and re-layouts: 2.34 us -> 0.01 us
    pallas_call x0 -> x1, Pallas kernels: none -> 0.85 us  [pair_call(): pl.pallas_call(pair_kernel, out_shape=jax.ShapeDtypeStruct(pay, jnp.float...]
where the time goes in v2:
time: 70 us; the launch traced here: 69.8 us
  blocking collectives  65 us (93%)
  Pallas kernels  4.14 us (6%)
    all_to_all x4, blocking collectives, exchange(): return lax.all_to_all(payload, ROW_COL, 0, 0, tiled=True)  65 us
    pallas_call x4, Pallas kernels, call(): pl.pallas_call(body, out_shape=[jax.ShapeDtypeStruct(s, jnp.float32) for...  3.29 us

profile of v2, /device:TPU:1, one launch (start us, length us, event | category | flops | bytes accessed | tf_op | source)
XLA Modules:
  0.0 69.8 jit_solution(8765049091783230476)
XLA Ops:
  0.6 0.0 copy-start
  0.6 0.9 %shard_map.50 = f32[256,128]{1,0:T(8,128)S(1)} custom-call(f32[1,96]{1,0:T(1,128)} %bitcast.18, f32[1,96]{1,0:T(1,128)} %bitcast.19, f32[192,6144]{1,0:T(8,128)} %refs_5_.1), custom_call_target="tpu_custom_call" | custom-call | bytes 18874368 | tf_op jit(solution)/shard_map/pallas_call | solution.py:166
  1.5 21.7 %all_to_all.44 = f32[128,2,128]{2,1,0:T(2,128)S(1)} all-to-all(f32[128,2,128]{2,1,0:T(2,128)S(1)} %bitcast.14), channel_id=1, replica_groups=mesh['row_0'=4,'row_1'=4,'row_2'=4,'col'=2] {'row_0','row_1','row_2','col'}, dimensions={0} | all-to-all | bytes 262144 | tf_op jit(solution)/shard_map/all_to_all | solution.py:183
  23.2 0.0 copy-done
  23.2 0.6 shard_map.51
  23.8 14.4 %all_to_all.45 = f32[128,2,128]{2,1,0:T(2,128)S(1)} all-to-all(f32[128,2,128]{2,1,0:T(2,128)S(1)} %bitcast.17), channel_id=1, replica_groups=mesh['row_0'=4,'row_1'=4,'row_2'=4,'col'=2] {'row_0','row_1','row_2','col'}, dimensions={0} | all-to-all | bytes 262144 | tf_op jit(solution)/shard_map/all_to_all | solution.py:183
  38.3 0.8 %shard_map.52 = (f32[96,128]{1,0:T(8,128)S(1)}, f32[8,128]{1,0:T(8,128)S(1)}, f32[256,128]{1,0:T(8,128)S(1)}) custom-call(f32[96,128]{1,0:T(8,128)S(1)} %get-tuple-element.11.refs_0_, f32[96,128]{1,0:T(8,128)S(1)} %get-tuple-element.12.refs_1_.refs_2_.refs_3_, f32[256,128]{1,0:T(8,128)S(1)} %bitcast.10, f32[8,128]{1,0:T(8,128)S(1)} %broadcast_in_dim.3.refs_3_, ...), custom_call_target="tpu_custom_call" | custom-call | tf_op jit(solution)/shard_map/pallas_call | solution.py:153
  39.1 14.4 %all_to_all.46 = f32[128,2,128]{2,1,0:T(2,128)S(1)} all-to-all(f32[128,2,128]{2,1,0:T(2,128)S(1)} %bitcast.15), channel_id=1, replica_groups=mesh['row_0'=4,'row_1'=4,'row_2'=4,'col'=2] {'row_0','row_1','row_2','col'}, dimensions={0} | all-to-all | bytes 262144 | tf_op jit(solution)/shard_map/all_to_all | solution.py:183
  53.5 0.8 %shard_map.53 = (f32[96,128]{1,0:T(8,128)S(1)}, f32[8,128]{1,0:T(8,128)S(1)}, f32[256,128]{1,0:T(8,128)S(1)}) custom-call(f32[96,128]{1,0:T(8,128)S(1)} %get-tuple-element.11.refs_0_, f32[96,128]{1,0:T(8,128)S(1)} %get-tuple-element.14.refs_1_, f32[96,128]{1,0:T(8,128)S(1)} %get-tuple-element.12.refs_1_.refs_2_.refs_3_, f32[256,128]{1,0:T(8,128)S(1)} %bitcast.11, ...), custom_call_target="tpu_custom_call" | custom-call | tf_op jit(solution)/shard_map/pallas_call | solution.py:153
  54.3 14.4 %all_to_all.47 = f32[128,2,128]{2,1,0:T(2,128)S(1)} all-to-all(f32[128,2,128]{2,1,0:T(2,128)S(1)} %bitcast.16), channel_id=1, replica_groups=mesh['row_0'=4,'row_1'=4,'row_2'=4,'col'=2] {'row_0','row_1','row_2','col'}, dimensions={0} | all-to-all | bytes 262144 | tf_op jit(solution)/shard_map/all_to_all | solution.py:183
  68.8 1.0 %shard_map.54 = (f32[4,96]{1,0:T(4,128)}, f32[2,3]{1,0:T(2,128)}) custom-call(f32[96,128]{1,0:T(8,128)S(1)} %get-tuple-element.11.refs_0_, f32[96,128]{1,0:T(8,128)S(1)} %get-tuple-element.14.refs_1_, f32[96,128]{1,0:T(8,128)S(1)} %get-tuple-element.17.refs_2_, f32[96,128]{1,0:T(8,128)S(1)} %get-tuple-element.12.refs_1_.refs_2_.refs_3_, ...), custom_call_target="tpu_custom_call" | custom-call | tf_op jit(solution)/shard_map/pallas_call | solution.py:153
  (1 shorter events, 0.0 us)
Async XLA Ops:
  0.6 22.5 %copy-start = (f32[192,6144]{1,0:T(8,128)S(1)}, f32[192,6144]{1,0:T(8,128)}, u32[]{:S(2)}) copy-start(f32[192,6144]{1,0:T(8,128)} %refs_5_.1) | copy-start | bytes 14155780

commit v3 on v2

--- a/solution.py
+++ b/solution.py
@@ -13,6 +13,9 @@
 LANES = 128
 ROW = ("row_0", "row_1", "row_2")
 ROW_COL = ("row_0", "row_1", "row_2", "col")
+ORDER = ("col", "row_2", "row_1", "row_0")
+SIDE = 4
+PLANE = SIDE * SIDE
 
 
 def total(x):
@@ -41,33 +44,45 @@
     return jnp.concatenate([a0, jnp.where(lane < 64, a1, r0), jnp.where(lane < 64, r0, r1)], axis=0)
 
 
-def gathered_image(g_ref, groups):
-    def rows(first):
-        return g_ref[pl.ds(first, groups, stride=8), :]
-
-    return join_192(
-        rows(0) + rows(2), rows(1) + rows(3), rows(4) + rows(6), rows(5) + rows(7)
-    )
-
-
-def product(vec, scale, m_ref, half_ref, pay_ref):
+def rows_of(g_ref, col, parity, part):
+    devices = g_ref.shape[0] // 2
+    return jnp.concatenate(
+        [
+            g_ref[pl.ds(col * devices + 2 * PLANE * (2 * u + parity) + part, PLANE, stride=2), :]
+            for u in range(SIDE // 2)
+        ],
+        axis=0,
+    )
+
+
+def gathered_image(g_ref):
+    a0, a1, b0, b1 = (
+        rows_of(g_ref, 0, parity, part) + rows_of(g_ref, 1, parity, part)
+        for parity in range(2)
+        for part in range(2)
+    )
+    return join_192(a0, a1, b0, b1)
+
+
+def product(vec, m_ref, vec_ref):
+    vec_ref[...] = vec
     groups = vec.shape[0] // 3
-    half = groups // 2
-    first = lax.axis_index("col") == 0
-    for k in range(3):
-        lo = vec[k * groups : k * groups + half]
-        hi = vec[k * groups + half : (k + 1) * groups]
-        half_ref[k * half : (k + 1) * half, :] = jnp.where(first, lo, hi)
+    shift = lax.axis_index("col") * (SIDE // 2)
     rows = m_ref.shape[0]
     acc = jnp.zeros((rows, LANES), jnp.float32)
     for t in range(m_ref.shape[1] // LANES):
-        v = half_ref[pl.ds((t % 3) * half + t // 3, 1), :]
+        group, k = t // 3, t % 3
+        z, y, u = group // (2 * SIDE), group // 2 % SIDE, group % 2
+        v = vec_ref[pl.ds(shift + (k * groups + u * PLANE + y * SIDE + z), 1), :]
         acc = acc + m_ref[:, t * LANES : (t + 1) * LANES] * v
     top = jnp.sum(acc[:LANES].T, axis=0, keepdims=True)
     low = jnp.concatenate([acc[LANES:], jnp.zeros((2 * LANES - rows, LANES), jnp.float32)], axis=0)
     bottom = jnp.sum(low.T, axis=0, keepdims=True)
     even = lax.broadcasted_iota(jnp.int32, (8, LANES), 0) % 2 == 0
-    tile = jnp.where(even, top, bottom) / scale
+    return jnp.where(even, top, bottom)
+
+
+def fill(pay_ref, tile):
     for i in range(pay_ref.shape[0] // 8):
         pay_ref[8 * i : 8 * i + 8, :] = tile
 
@@ -86,27 +101,27 @@
     pair_ref[0:1, 0:width] = s_got[...]
     pair_ref[1:2, 0:width] = d_got[...]
     even = lax.broadcasted_iota(jnp.int32, (8, LANES), 0) % 2 == 0
-    tile = jnp.where(even, pair_ref[0:1, :], pair_ref[1:2, :])
-    for i in range(pay_ref.shape[0] // 8):
-        pay_ref[8 * i : 8 * i + 8, :] = tile
-
-
-def first_kernel(g_ref, m_ref, q_ref, d_ref, pay_ref, half_ref):
-    groups = g_ref.shape[0] // 8
-    start = join_96([g_ref[pl.ds(2 * j, groups, stride=8), :] for j in range(4)])
-    d_ref[...] = join_96([g_ref[pl.ds(2 * j + 1, groups, stride=8), :] for j in range(4)])
-    norm = jnp.sqrt(total(start * start))
-    q_ref[...] = start / norm
-    product(start, norm, m_ref, half_ref, pay_ref)
-
-
-def orthogonal(g_ref, q_refs, d_ref):
-    groups = g_ref.shape[0] // 8
-    image = gathered_image(g_ref, groups) + d_ref[...] * q_refs[-1][...]
+    fill(pay_ref, jnp.where(even, pair_ref[0:1, :], pair_ref[1:2, :]))
+
+
+def first_kernel(g_ref, m_ref, q_ref, d_ref, tile_ref, pay_ref, vec_ref):
+    start, diag = (
+        join_96([rows_of(g_ref, j % 2, j // 2, part) for j in range(4)]) for part in range(2)
+    )
+    d_ref[...] = diag
+    tile = product(start, m_ref, vec_ref)
+    scale = 1.0 / jnp.sqrt(total(start * start))
+    q_ref[...] = start * scale
+    tile = tile * scale
+    tile_ref[...] = tile
+    fill(pay_ref, tile)
+
+
+def orthogonal(image, q_refs):
     dots = [total(q[...] * image) for q in q_refs]
     for h, q in zip(dots, q_refs):
         image = image - h * q[...]
-    return image, dots[-1], jnp.sqrt(total(image * image))
+    return image, dots, jnp.sqrt(total(image * image))
 
 
 def put(coef, row, col, value):
@@ -116,25 +131,34 @@
 
 
 def middle_kernel(k, *refs):
-    q_refs = refs[: k + 1]
-    d_ref, g_ref, c_ref, m_ref, next_ref, c_out, pay_ref, half_ref = refs[k + 1 :]
-    image, alpha, beta = orthogonal(g_ref, q_refs, d_ref)
-    next_ref[...] = image / beta
-    c_out[...] = put(put(c_ref[...], 0, k, alpha), 1, k, beta)
-    product(image, beta, m_ref, half_ref, pay_ref)
+    q_refs, tile_refs = refs[: k + 1], refs[k + 1 : 2 * k + 2]
+    d_ref, g_ref, c_ref, m_ref, next_ref, c_out, tile_ref, pay_ref, vec_ref = refs[2 * k + 2 :]
+    image = gathered_image(g_ref) + d_ref[...] * q_refs[-1][...]
+    tile = product(image, m_ref, vec_ref)
+    image, dots, beta = orthogonal(image, q_refs)
+    scale = 1.0 / beta
+    next_ref[...] = image * scale
+    c_out[...] = put(put(c_ref[...], 0, k, dots[-1]), 1, k, beta)
+    for h, t in zip(dots, tile_refs):
+        tile = tile - h * t[...]
+    tile = tile * scale
+    tile_ref[...] = tile
+    fill(pay_ref, tile)
 
 
 def last_kernel(k, full_dim, *refs):
     q_refs = refs[: k + 1]
     d_ref, g_ref, c_ref, basis_ref, c_out, last_ref, piece_ref = refs[k + 1 :]
-    image, alpha, beta = orthogonal(g_ref, q_refs, d_ref)
-    last_ref[...] = image / beta
+    image = gathered_image(g_ref) + d_ref[...] * q_refs[-1][...]
+    image, dots, beta = orthogonal(image, q_refs)
+    alpha = dots[-1]
+    last_ref[...] = image * (1.0 / beta)
     coef = put(put(c_ref[...], 0, k, alpha), 1, k, beta)
     c_out[...] = coef[: c_out.shape[0], : c_out.shape[1]]
     groups = image.shape[0] // 3
-    index = lax.axis_index(ROW_COL)
-    group = index // 4
-    place = index % 4
+    x = lax.axis_index("row_2")
+    group = x // 2 * PLANE + lax.axis_index("row_1") * SIDE + lax.axis_index("row_0")
+    place = x % 2 * 2 + lax.axis_index("col")
     for j in range(3):
         for v, q in enumerate((*q_refs, last_ref)):
             piece_ref[8 * j + v : 8 * j + v + 1, :] = q[pl.ds(j * groups + group, 1), :]
@@ -180,7 +204,7 @@
 
 
 def exchange(payload):
-    return lax.all_to_all(payload, ROW_COL, 0, 0, tiled=True)
+    return lax.all_to_all(payload, ORDER, 0, 0, tiled=True)
 
 
 def local(matrix, diagonal, start):
@@ -188,26 +212,28 @@
     tile_len = start.shape[0]
     full_dim = tile_len * devices
     dense = (full_dim // LANES, LANES)
-    half = (full_dim // LANES // 2, LANES)
     pay = (2 * devices, LANES)
     payload = pair_call(pay, start.reshape(1, -1), diagonal.reshape(1, -1), matrix)
     gathered = exchange(payload)
-    q, diag, payload = call(first_kernel, [dense, dense, pay], [half], gathered, matrix)
-    basis = [q]
-    coef = jnp.zeros((8, LANES), jnp.float32)
+    tile = (8, LANES)
+    q, diag, part, payload = call(first_kernel, [dense, dense, tile, pay], [dense], gathered, matrix)
+    basis, parts = [q], [part]
+    coef = jnp.zeros(tile, jnp.float32)
     for k in range(ITERS - 1):
         gathered = exchange(payload)
-        q, coef, payload = call(
+        q, coef, part, payload = call(
             functools.partial(middle_kernel, k),
-            [dense, (8, LANES), pay],
-            [half],
+            [dense, tile, tile, pay],
+            [dense],
             *basis,
+            *parts,
             diag,
             gathered,
             coef,
             matrix,
         )
         basis.append(q)
+        parts.append(part)
     gathered = exchange(payload)
     return tuple(
         call(

time: 70 us -> 69.3 us (0.990)
  blocking collectives: 65 us -> 64.1 us
    all_to_all x4, blocking collectives: 65 us -> 64.1 us  [exchange(): return lax.all_to_all(payload, ORDER, 0, 0, tiled=True)]
where the time goes in v3:
time: 69.3 us; the launch traced here: 69.1 us
  blocking collectives  64.1 us (92%)
  Pallas kernels  4.31 us (6%)
    all_to_all x4, blocking collectives, exchange(): return lax.all_to_all(payload, ORDER, 0, 0, tiled=True)  64.1 us
    pallas_call x4, Pallas kernels, call(): pl.pallas_call(body, out_shape=[jax.ShapeDtypeStruct(s, jnp.float32) for...  3.45 us

profile of v3, /device:TPU:1, one launch (start us, length us, event | category | flops | bytes accessed | tf_op | source)
XLA Modules:
  0.0 69.1 jit_solution(13932314654807760578)
XLA Ops:
  0.6 0.0 copy-start
  0.6 0.9 %shard_map.50 = f32[256,128]{1,0:T(8,128)S(1)} custom-call(f32[1,96]{1,0:T(1,128)} %bitcast.18, f32[1,96]{1,0:T(1,128)} %bitcast.19, f32[192,6144]{1,0:T(8,128)} %refs_7_.1), custom_call_target="tpu_custom_call" | custom-call | bytes 18874368 | tf_op jit(solution)/shard_map/pallas_call | solution.py:190
  1.5 21.4 %all_to_all.44 = f32[128,2,128]{2,1,0:T(2,128)S(1)} all-to-all(f32[128,2,128]{2,1,0:T(2,128)S(1)} %bitcast.14), channel_id=1, replica_groups=mesh['row_0'=4,'row_1'=4,'row_2'=4,'col'=2] {'col','row_2','row_1','row_0'}, dimensions={0} | all-to-all | bytes 262144 | tf_op jit(solution)/shard_map/all_to_all | solution.py:207
  22.9 0.0 copy-done
  22.9 0.6 shard_map.51
  23.5 14.3 %all_to_all.45 = f32[128,2,128]{2,1,0:T(2,128)S(1)} all-to-all(f32[128,2,128]{2,1,0:T(2,128)S(1)} %bitcast.17), channel_id=1, replica_groups=mesh['row_0'=4,'row_1'=4,'row_2'=4,'col'=2] {'col','row_2','row_1','row_0'}, dimensions={0} | all-to-all | bytes 262144 | tf_op jit(solution)/shard_map/all_to_all | solution.py:207
  37.7 0.6 shard_map.52
  38.4 14.3 %all_to_all.46 = f32[128,2,128]{2,1,0:T(2,128)S(1)} all-to-all(f32[128,2,128]{2,1,0:T(2,128)S(1)} %bitcast.16), channel_id=1, replica_groups=mesh['row_0'=4,'row_1'=4,'row_2'=4,'col'=2] {'col','row_2','row_1','row_0'}, dimensions={0} | all-to-all | bytes 262144 | tf_op jit(solution)/shard_map/all_to_all | solution.py:207
  52.6 1.2 %shard_map.53 = (f32[96,128]{1,0:T(8,128)S(1)}, f32[8,128]{1,0:T(8,128)S(1)}, f32[8,128]{1,0:T(8,128)}, f32[256,128]{1,0:T(8,128)S(1)}) custom-call(f32[96,128]{1,0:T(8,128)S(1)} %get-tuple-element.13.refs_0_, f32[96,128]{1,0:T(8,128)S(1)} %get-tuple-element.17.refs_1_, f32[8,128]{1,0:T(8,128)S(1)} %get-tuple-element.14.refs_1_.refs_2_, ...), custom_call_target="tpu_custom_call" | custom-call | tf_op jit(solution)/shard_map/pallas_call | solution.py:177
  53.9 14.3 %all_to_all.47 = f32[128,2,128]{2,1,0:T(2,128)S(1)} all-to-all(f32[128,2,128]{2,1,0:T(2,128)S(1)} %bitcast.15), channel_id=1, replica_groups=mesh['row_0'=4,'row_1'=4,'row_2'=4,'col'=2] {'col','row_2','row_1','row_0'}, dimensions={0} | all-to-all | bytes 262144 | tf_op jit(solution)/shard_map/all_to_all | solution.py:207
  68.1 1.0 %shard_map.54 = (f32[4,96]{1,0:T(4,128)}, f32[2,3]{1,0:T(2,128)}) custom-call(f32[96,128]{1,0:T(8,128)S(1)} %get-tuple-element.13.refs_0_, f32[96,128]{1,0:T(8,128)S(1)} %get-tuple-element.17.refs_1_, f32[96,128]{1,0:T(8,128)S(1)} %get-tuple-element.21.refs_2_, f32[96,128]{1,0:T(8,128)S(1)} %get-tuple-element.15.refs_2_.refs_4_.refs_3_, ...), custom_call_target="tpu_custom_call" | custom-call | tf_op jit(solution)/shard_map/pallas_call | solution.py:177
  (1 shorter events, 0.0 us)
Async XLA Ops:
  0.6 22.2 %copy-start = (f32[192,6144]{1,0:T(8,128)S(1)}, f32[192,6144]{1,0:T(8,128)}, u32[]{:S(2)}) copy-start(f32[192,6144]{1,0:T(8,128)} %refs_7_.1) | copy-start | bytes 14155780

commit v4 on v3

--- a/solution.py
+++ b/solution.py
@@ -65,8 +65,9 @@
 
 
 def product(vec, m_ref, vec_ref):
-    vec_ref[...] = vec
-    groups = vec.shape[0] // 3
+    if vec is not None:
+        vec_ref[...] = vec
+    groups = vec_ref.shape[0] // 3
     shift = lax.axis_index("col") * (SIDE // 2)
     rows = m_ref.shape[0]
     acc = jnp.zeros((rows, LANES), jnp.float32)
@@ -117,11 +118,14 @@
     fill(pay_ref, tile)
 
 
-def orthogonal(image, q_refs):
-    dots = [total(q[...] * image) for q in q_refs]
+def dots_of(image, q_refs):
+    return [total(q[...] * image) for q in q_refs]
+
+
+def orthogonal(image, dots, q_refs):
     for h, q in zip(dots, q_refs):
         image = image - h * q[...]
-    return image, dots, jnp.sqrt(total(image * image))
+    return image, jnp.sqrt(total(image * image))
 
 
 def put(coef, row, col, value):
@@ -132,17 +136,20 @@
 
 def middle_kernel(k, *refs):
     q_refs, tile_refs = refs[: k + 1], refs[k + 1 : 2 * k + 2]
-    d_ref, g_ref, c_ref, m_ref, next_ref, c_out, tile_ref, pay_ref, vec_ref = refs[2 * k + 2 :]
+    d_ref, g_ref, c_ref, m_ref, next_ref, c_out, pay_ref, *out_refs, vec_ref = refs[2 * k + 2 :]
     image = gathered_image(g_ref) + d_ref[...] * q_refs[-1][...]
-    tile = product(image, m_ref, vec_ref)
-    image, dots, beta = orthogonal(image, q_refs)
+    dots = dots_of(image, q_refs)
+    vec_ref[...] = image
+    image, beta = orthogonal(image, dots, q_refs)
+    tile = product(None, m_ref, vec_ref)
     scale = 1.0 / beta
     next_ref[...] = image * scale
     c_out[...] = put(put(c_ref[...], 0, k, dots[-1]), 1, k, beta)
     for h, t in zip(dots, tile_refs):
         tile = tile - h * t[...]
     tile = tile * scale
-    tile_ref[...] = tile
+    for tile_ref in out_refs:
+        tile_ref[...] = tile
     fill(pay_ref, tile)
 
 
@@ -150,10 +157,10 @@
     q_refs = refs[: k + 1]
     d_ref, g_ref, c_ref, basis_ref, c_out, last_ref, piece_ref = refs[k + 1 :]
     image = gathered_image(g_ref) + d_ref[...] * q_refs[-1][...]
-    image, dots, beta = orthogonal(image, q_refs)
-    alpha = dots[-1]
-    last_ref[...] = image * (1.0 / beta)
-    coef = put(put(c_ref[...], 0, k, alpha), 1, k, beta)
+    dots = dots_of(image, q_refs)
+    image, beta = orthogonal(image, dots, q_refs)
+    last_ref[...] = image
+    coef = put(put(c_ref[...], 0, k, dots[-1]), 1, k, beta)
     c_out[...] = coef[: c_out.shape[0], : c_out.shape[1]]
     groups = image.shape[0] // 3
     x = lax.axis_index("row_2")
@@ -168,7 +175,8 @@
     two = jnp.where(lane < 64, pltpu.roll(b, 64, 1), pltpu.roll(c, 64, 1))
     three = pltpu.roll(c, 96, 1)
     out = jnp.where(place == 0, a, jnp.where(place == 1, one, jnp.where(place == 2, two, three)))
-    out = out * jnp.float32(math.sqrt(full_dim))
+    newest = lax.broadcasted_iota(jnp.int32, out.shape, 0) == len(q_refs)
+    out = out * jnp.float32(math.sqrt(full_dim)) * jnp.where(newest, 1.0 / beta, 1.0)
     basis_ref[...] = out[: basis_ref.shape[0], : basis_ref.shape[1]]
 
 
@@ -221,9 +229,9 @@
     coef = jnp.zeros(tile, jnp.float32)
     for k in range(ITERS - 1):
         gathered = exchange(payload)
-        q, coef, part, payload = call(
+        q, coef, payload, *part = call(
             functools.partial(middle_kernel, k),
-            [dense, tile, tile, pay],
+            [dense, tile, pay] + [tile] * (k < ITERS - 2),
             [dense],
             *basis,
             *parts,
@@ -233,7 +241,7 @@
             matrix,
         )
         basis.append(q)
-        parts.append(part)
+        parts += part
     gathered = exchange(payload)
     return tuple(
         call(

time: 69.3 us -> 68.4 us (0.987)
  Pallas kernels: 4.31 us -> 3.37 us
    pallas_call x4, Pallas kernels: 3.45 us -> 2.51 us  [call(): pl.pallas_call(body, out_shape=[jax.ShapeDtypeStruct(s, jnp.float32) for...]
where the time goes in v4:
time: 68.4 us; the launch traced here: 68.2 us
  blocking collectives  64.2 us (94%)
  Pallas kernels  3.37 us (5%)
    all_to_all x4, blocking collectives, exchange(): return lax.all_to_all(payload, ORDER, 0, 0, tiled=True)  64.2 us
    pallas_call x4, Pallas kernels, call(): pl.pallas_call(body, out_shape=[jax.ShapeDtypeStruct(s, jnp.float32) for...  2.51 us

profile of v4, /device:TPU:1, one launch (start us, length us, event | category | flops | bytes accessed | tf_op | source)
XLA Modules:
  0.0 68.2 jit_solution(7344214779754783430)
XLA Ops:
  0.6 0.0 copy-start
  0.6 0.9 %shard_map.50 = f32[256,128]{1,0:T(8,128)S(1)} custom-call(f32[1,96]{1,0:T(1,128)} %bitcast.18, f32[1,96]{1,0:T(1,128)} %bitcast.19, f32[192,6144]{1,0:T(8,128)} %refs_7_.1), custom_call_target="tpu_custom_call" | custom-call | bytes 18874368 | tf_op jit(solution)/shard_map/pallas_call | solution.py:198
  1.5 21.4 %all_to_all.44 = f32[128,2,128]{2,1,0:T(2,128)S(1)} all-to-all(f32[128,2,128]{2,1,0:T(2,128)S(1)} %bitcast.14), channel_id=1, replica_groups=mesh['row_0'=4,'row_1'=4,'row_2'=4,'col'=2] {'col','row_2','row_1','row_0'}, dimensions={0} | all-to-all | bytes 262144 | tf_op jit(solution)/shard_map/all_to_all | solution.py:215
  22.9 0.0 copy-done
  22.9 0.5 shard_map.51
  23.4 14.3 %all_to_all.45 = f32[128,2,128]{2,1,0:T(2,128)S(1)} all-to-all(f32[128,2,128]{2,1,0:T(2,128)S(1)} %bitcast.17), channel_id=1, replica_groups=mesh['row_0'=4,'row_1'=4,'row_2'=4,'col'=2] {'col','row_2','row_1','row_0'}, dimensions={0} | all-to-all | bytes 262144 | tf_op jit(solution)/shard_map/all_to_all | solution.py:215
  37.6 0.5 shard_map.52
  38.2 14.3 %all_to_all.46 = f32[128,2,128]{2,1,0:T(2,128)S(1)} all-to-all(f32[128,2,128]{2,1,0:T(2,128)S(1)} %bitcast.16), channel_id=1, replica_groups=mesh['row_0'=4,'row_1'=4,'row_2'=4,'col'=2] {'col','row_2','row_1','row_0'}, dimensions={0} | all-to-all | bytes 262144 | tf_op jit(solution)/shard_map/all_to_all | solution.py:215
  52.5 0.5 shard_map.53
  53.0 14.3 %all_to_all.47 = f32[128,2,128]{2,1,0:T(2,128)S(1)} all-to-all(f32[128,2,128]{2,1,0:T(2,128)S(1)} %bitcast.15), channel_id=1, replica_groups=mesh['row_0'=4,'row_1'=4,'row_2'=4,'col'=2] {'col','row_2','row_1','row_0'}, dimensions={0} | all-to-all | bytes 262144 | tf_op jit(solution)/shard_map/all_to_all | solution.py:215
  67.3 0.9 %shard_map.54 = (f32[4,96]{1,0:T(4,128)}, f32[2,3]{1,0:T(2,128)}) custom-call(f32[96,128]{1,0:T(8,128)S(1)} %get-tuple-element.13.refs_0_, f32[96,128]{1,0:T(8,128)S(1)} %get-tuple-element.17.refs_1_, f32[96,128]{1,0:T(8,128)S(1)} %get-tuple-element.21.refs_2_, f32[96,128]{1,0:T(8,128)S(1)} %get-tuple-element.15.refs_2_.refs_4_.refs_3_, ...), custom_call_target="tpu_custom_call" | custom-call | tf_op jit(solution)/shard_map/pallas_call | solution.py:185
  (1 shorter events, 0.0 us)
Async XLA Ops:
  0.6 22.2 %copy-start = (f32[192,6144]{1,0:T(8,128)S(1)}, f32[192,6144]{1,0:T(8,128)}, u32[]{:S(2)}) copy-start(f32[192,6144]{1,0:T(8,128)} %refs_7_.1) | copy-start | bytes 14155780

commit v5 on v4

--- a/solution.py
+++ b/solution.py
@@ -13,9 +13,7 @@
 LANES = 128
 ROW = ("row_0", "row_1", "row_2")
 ROW_COL = ("row_0", "row_1", "row_2", "col")
-ORDER = ("col", "row_2", "row_1", "row_0")
-SIDE = 4
-PLANE = SIDE * SIDE
+ORDER = ("col", "row_0", "row_1", "row_2")
 
 
 def total(x):
@@ -46,13 +44,7 @@
 
 def rows_of(g_ref, col, parity, part):
     devices = g_ref.shape[0] // 2
-    return jnp.concatenate(
-        [
-            g_ref[pl.ds(col * devices + 2 * PLANE * (2 * u + parity) + part, PLANE, stride=2), :]
-            for u in range(SIDE // 2)
-        ],
-        axis=0,
-    )
+    return g_ref[pl.ds(col * devices + 2 * parity + part, devices // 4, stride=4), :]
 
 
 def gathered_image(g_ref):
@@ -68,13 +60,11 @@
     if vec is not None:
         vec_ref[...] = vec
     groups = vec_ref.shape[0] // 3
-    shift = lax.axis_index("col") * (SIDE // 2)
+    shift = lax.axis_index("col") * (groups // 2)
     rows = m_ref.shape[0]
     acc = jnp.zeros((rows, LANES), jnp.float32)
     for t in range(m_ref.shape[1] // LANES):
-        group, k = t // 3, t % 3
-        z, y, u = group // (2 * SIDE), group // 2 % SIDE, group % 2
-        v = vec_ref[pl.ds(shift + (k * groups + u * PLANE + y * SIDE + z), 1), :]
+        v = vec_ref[pl.ds(shift + (t % 3 * groups + t // 3), 1), :]
         acc = acc + m_ref[:, t * LANES : (t + 1) * LANES] * v
     top = jnp.sum(acc[:LANES].T, axis=0, keepdims=True)
     low = jnp.concatenate([acc[LANES:], jnp.zeros((2 * LANES - rows, LANES), jnp.float32)], axis=0)
@@ -163,9 +153,9 @@
     coef = put(put(c_ref[...], 0, k, dots[-1]), 1, k, beta)
     c_out[...] = coef[: c_out.shape[0], : c_out.shape[1]]
     groups = image.shape[0] // 3
-    x = lax.axis_index("row_2")
-    group = x // 2 * PLANE + lax.axis_index("row_1") * SIDE + lax.axis_index("row_0")
-    place = x % 2 * 2 + lax.axis_index("col")
+    row = lax.axis_index(ROW)
+    group = row // 2
+    place = row % 2 * 2 + lax.axis_index("col")
     for j in range(3):
         for v, q in enumerate((*q_refs, last_ref)):
             piece_ref[8 * j + v : 8 * j + v + 1, :] = q[pl.ds(j * groups + group, 1), :]

time: 68.4 us -> 67.2 us (0.982)
  blocking collectives: 64.2 us -> 62.8 us
    all_to_all x4, blocking collectives: 64.2 us -> 62.8 us  [exchange(): return lax.all_to_all(payload, ORDER, 0, 0, tiled=True)]
where the time goes in v5:
time: 67.2 us; the launch traced here: 67 us
  blocking collectives  62.8 us (93%)
  Pallas kernels  3.54 us (5%)
    all_to_all x4, blocking collectives, exchange(): return lax.all_to_all(payload, ORDER, 0, 0, tiled=True)  62.8 us
    pallas_call x4, Pallas kernels, call(): pl.pallas_call(body, out_shape=[jax.ShapeDtypeStruct(s, jnp.float32) for...  2.68 us

profile of v5, /device:TPU:1, one launch (start us, length us, event | category | flops | bytes accessed | tf_op | source)
XLA Modules:
  0.0 67.0 jit_solution(17434292359949264877)
XLA Ops:
  0.6 0.0 copy-start
  0.6 0.9 %shard_map.50 = f32[256,128]{1,0:T(8,128)S(1)} custom-call(f32[1,96]{1,0:T(1,128)} %bitcast.18, f32[1,96]{1,0:T(1,128)} %bitcast.19, f32[192,6144]{1,0:T(8,128)} %refs_7_.1), custom_call_target="tpu_custom_call" | custom-call | bytes 18874368 | tf_op jit(solution)/shard_map/pallas_call | solution.py:188
  1.5 21.5 %all_to_all.44 = f32[128,2,128]{2,1,0:T(2,128)S(1)} all-to-all(f32[128,2,128]{2,1,0:T(2,128)S(1)} %bitcast.14), channel_id=1, replica_groups=mesh['row_0'=4,'row_1'=4,'row_2'=4,'col'=2] {'col','row_0','row_1','row_2'}, dimensions={0} | all-to-all | bytes 262144 | tf_op jit(solution)/shard_map/all_to_all | solution.py:205
  23.0 0.0 copy-done
  23.0 0.6 shard_map.51
  23.6 13.8 %all_to_all.45 = f32[128,2,128]{2,1,0:T(2,128)S(1)} all-to-all(f32[128,2,128]{2,1,0:T(2,128)S(1)} %bitcast.17), channel_id=1, replica_groups=mesh['row_0'=4,'row_1'=4,'row_2'=4,'col'=2] {'col','row_0','row_1','row_2'}, dimensions={0} | all-to-all | bytes 262144 | tf_op jit(solution)/shard_map/all_to_all | solution.py:205
  37.4 0.6 shard_map.52
  38.0 13.8 %all_to_all.46 = f32[128,2,128]{2,1,0:T(2,128)S(1)} all-to-all(f32[128,2,128]{2,1,0:T(2,128)S(1)} %bitcast.16), channel_id=1, replica_groups=mesh['row_0'=4,'row_1'=4,'row_2'=4,'col'=2] {'col','row_0','row_1','row_2'}, dimensions={0} | all-to-all | bytes 262144 | tf_op jit(solution)/shard_map/all_to_all | solution.py:205
  51.7 0.6 shard_map.53
  52.3 13.8 %all_to_all.47 = f32[128,2,128]{2,1,0:T(2,128)S(1)} all-to-all(f32[128,2,128]{2,1,0:T(2,128)S(1)} %bitcast.15), channel_id=1, replica_groups=mesh['row_0'=4,'row_1'=4,'row_2'=4,'col'=2] {'col','row_0','row_1','row_2'}, dimensions={0} | all-to-all | bytes 262144 | tf_op jit(solution)/shard_map/all_to_all | solution.py:205
  66.1 0.9 %shard_map.54 = (f32[4,96]{1,0:T(4,128)}, f32[2,3]{1,0:T(2,128)}) custom-call(f32[96,128]{1,0:T(8,128)S(1)} %get-tuple-element.13.refs_0_, f32[96,128]{1,0:T(8,128)S(1)} %get-tuple-element.17.refs_1_, f32[96,128]{1,0:T(8,128)S(1)} %get-tuple-element.21.refs_2_, f32[96,128]{1,0:T(8,128)S(1)} %get-tuple-element.15.refs_2_.refs_4_.refs_3_, ...), custom_call_target="tpu_custom_call" | custom-call | tf_op jit(solution)/shard_map/pallas_call | solution.py:175
  (1 shorter events, 0.0 us)
Async XLA Ops:
  0.6 22.4 %copy-start = (f32[192,6144]{1,0:T(8,128)S(1)}, f32[192,6144]{1,0:T(8,128)}, u32[]{:S(2)}) copy-start(f32[192,6144]{1,0:T(8,128)} %refs_7_.1) | copy-start | bytes 14155780
